TPU v7x, 32 devices: a whole 2x2x4 slice. The times are simulated.
32 devices in a mesh: depth: 4 (over y, x), screen: 8 (over z, core).
Axes of the slice: x: 2, y: 2, z: 4, core: 2. Of those that a mesh axis runs over, the one named last changes fastest.
Arguments:
- voxel_bins: int32 [32, 256, 2048], P('depth', None, 'screen'), may hold values from 0 to 255
- colors: bfloat16 [3, 256], replicated, may hold values from 0 to 2
- opacity: bfloat16 [256], replicated, may hold values from 0 to 1
- slab_order: int32 [8, 4], replicated, may hold values from 0 to 3, each once within a row
Outputs:
- image: float32 [4, 256, 2048], P(None, ('depth', 'screen'))
Inputs may be any that keep to these rules, and one draw needn't show every extreme that they name: `slab_order`: every row is a permutation of 0 to 3.
All inputs are finite; a program needn't handle non-finite values.
Results may differ from a plain program's by a relative error of at most 0.0003.
Values sent between devices are 32-bit elements; how exact they have to be, the bound alone decides.
A program may use at most 64 MiB of HBM per device.

v0:
```python
import functools

import jax
import jax.numpy as jnp
from jax import lax
from jax.experimental import pallas as pl
from jax.experimental.pallas import tpu as pltpu
from jax.sharding import PartitionSpec as P

extinction = 3.0
lanes = 128
MESH = pl.DeviceIdType.MESH


def flip(index, mask, count):
    result = index
    bit = 1
    while bit < count:
        if isinstance(mask, int):
            if mask & bit:
                result = result + bit * (1 - 2 * lax.rem(lax.div(index, bit), 2))
        else:
            mine = lax.rem(lax.div(index, bit), 2)
            other = lax.rem(lax.div(mask, bit), 2)
            result = result + bit * other * (1 - 2 * mine)
        bit *= 2
    return result


def kernel(
    sizes,
    order_ref,
    bins_hbm,
    colors_ref,
    opacity_ref,
    out_ref,
    bins,
    sent,
    own,
    arrived,
    merged,
    bins_sem,
    send_sem,
    recv_sem,
    row_send_sem,
    row_recv_sem,
    ready_sem,
    go_sem,
):
    depth_count, tile_count, samples, unit_rows, units, owners, rows_each, cols, rate = sizes
    depth = lax.axis_index("depth")
    tile = lax.axis_index("screen")
    own_unit = lax.div(tile, owners)
    own_place = lax.rem(tile, owners)
    steps = list(range(units - 1, -1, -1))
    peers = [depth_count - 1] + list(range(1, depth_count - 1)) + [0]

    barrier = pltpu.get_barrier_semaphore()
    hub = depth == 0
    for mask in range(1, depth_count):
        peer = flip(depth, mask, depth_count)

        @pl.when(peer != 0)
        def _():
            pl.semaphore_signal(barrier, inc=1, device_id=(peer, tile), device_id_type=MESH)

    def meet_depth():
        @pl.when(jnp.logical_not(hub))
        def _():
            pl.semaphore_wait(barrier, depth_count - 1)
            pl.semaphore_signal(ready_sem, inc=1, device_id=(0, tile), device_id_type=MESH)

        @pl.when(hub)
        def _():
            pl.semaphore_wait(ready_sem, depth_count - 1)
            for mask in range(1, tile_count):
                pl.semaphore_signal(
                    barrier,
                    inc=1,
                    device_id=(0, flip(tile, mask, tile_count)),
                    device_id_type=MESH,
                )

    def meet_tiles():
        @pl.when(hub)
        def _():
            pl.semaphore_wait(barrier, tile_count - 1)
            for mask in range(1, depth_count):
                pl.semaphore_signal(go_sem, inc=1, device_id=(mask, tile), device_id_type=MESH)

        @pl.when(jnp.logical_not(hub))
        def _():
            pl.semaphore_wait(go_sem, 1)

    def fetch(step, mask):
        row = (flip(depth, mask, depth_count) * units + flip(own_unit, step, units)) * unit_rows
        row = pl.multiple_of(row, unit_rows)
        return pltpu.make_async_copy(
            bins_hbm.at[:, pl.ds(row, unit_rows), :],
            bins.at[step, mask],
            bins_sem.at[step, mask],
        )

    for step in steps:
        for mask in peers:
            if mask:
                fetch(step, mask).start()
    for step in steps:
        fetch(step, 0).start()

    density = opacity_ref[...].astype(jnp.float32).reshape(1, -1)
    weight = 1.0 - jnp.exp(-rate * density)
    shades = weight * colors_ref[...].astype(jnp.float32)
    table = [shades[c : c + 1] for c in range(3)] + [weight]
    bin_count = weight.shape[1]
    parts = [
        [jnp.broadcast_to(row[:, at : at + lanes], (8, lanes)) for at in range(0, bin_count, lanes)]
        for row in table
    ]

    def march(step, mask, target):
        for row in range(0, unit_rows, 8):
            for col in range(0, cols, lanes):
                clear = None
                total = None
                for j in range(samples):
                    index = bins[step, mask, j, row : row + 8, col : col + lanes]
                    low = lax.rem(index, lanes) if lanes & (lanes - 1) else index & (lanes - 1)
                    values = []
                    for part in parts:
                        value = jnp.take_along_axis(part[0], low, axis=1, mode="promise_in_bounds")
                        for n in range(1, len(part)):
                            other = jnp.take_along_axis(
                                part[n], low, axis=1, mode="promise_in_bounds"
                            )
                            value = jnp.where(index >= n * lanes, other, value)
                        values.append(value)
                    if total is None:
                        total = values
                        clear = 1.0 - values[3]
                    else:
                        seen = clear * values[3]
                        total = [t + clear * v for t, v in zip(total[:3], values[:3])] + [
                            total[3] + seen
                        ]
                        clear = clear - seen
                for c in range(4):
                    target[c, row : row + 8, col : col + lanes] = total[c]

    def send(step, mask):
        return pltpu.make_async_remote_copy(
            src_ref=sent.at[step, mask - 1],
            dst_ref=arrived.at[step, mask - 1],
            send_sem=send_sem.at[step, mask - 1],
            recv_sem=recv_sem.at[step, mask - 1],
            device_id=(flip(depth, mask, depth_count), tile),
            device_id_type=MESH,
        )

    def send_row(step, low):
        mask = step * owners + low
        place = flip(own_place, low, owners)
        there = pl.ds(pl.multiple_of(tile * cols, lanes), cols)
        return pltpu.make_async_remote_copy(
            src_ref=merged.at[step, place],
            dst_ref=out_ref.at[:, :, there],
            send_sem=row_send_sem.at[mask],
            recv_sem=row_recv_sem.at[mask],
            device_id=(depth, flip(tile, mask, tile_count)),
            device_id_type=MESH,
        )

    def take_row(mask):
        here = pl.ds(pl.multiple_of(flip(tile, mask, tile_count) * cols, lanes), cols)
        return pltpu.make_async_remote_copy(
            src_ref=merged.at[0, 0],
            dst_ref=out_ref.at[:, :, here],
            send_sem=row_send_sem.at[mask],
            recv_sem=row_recv_sem.at[mask],
            device_id=(depth, flip(tile, mask, tile_count)),
            device_id_type=MESH,
        )

    def feed(n):
        step = units - 1 - n
        for mask in peers:
            if mask:
                fetch(step, mask).wait()
                march(step, mask, sent.at[step, mask - 1])

        @pl.when(n == 0)
        def _():
            meet_depth()

        for mask in peers:
            if mask:
                send(step, mask).start()

    place_of = [order_ref[flip(depth, mask, depth_count), tile] for mask in range(depth_count)]
    ahead = [
        [jnp.where(place_of[j] < place_of[i], 1.0, 0.0) for j in range(depth_count)]
        for i in range(depth_count)
    ]

    def blend(n):
        step = units - 1 - n
        fetch(step, 0).wait()
        march(step, 0, own.at[step])

        @pl.when(n == 0)
        def _():
            meet_tiles()

        for mask in peers:
            if mask:
                send(step, mask).wait_recv()
        for row in range(0, unit_rows, 8):
            for col in range(0, cols, lanes):
                window = (slice(row, row + 8), slice(col, col + lanes))
                pieces = [
                    own[(step, slice(None)) + window]
                    if mask == 0
                    else arrived[(step, mask - 1, slice(None)) + window]
                    for mask in range(depth_count)
                ]
                total = None
                for i in range(depth_count):
                    front = None
                    for j in range(depth_count):
                        if j != i:
                            passed = 1.0 - ahead[i][j] * pieces[j][3]
                            front = passed if front is None else front * passed
                    lit = [pieces[i][c] if front is None else pieces[i][c] * front for c in range(4)]
                    total = lit if total is None else [t + v for t, v in zip(total, lit)]
                for c in range(4):
                    if owners == 1:
                        merged[step, 0, c, row : row + 8, col : col + lanes] = total[c]
                    else:
                        for place in range(owners):
                            merged[step, place, c, :, col : col + lanes] = total[c][
                                place * rows_each : (place + 1) * rows_each
                            ]
        for low in range(owners - 1, 0, -1):
            send_row(step, low).start()

        @pl.when(step > 0)
        def _():
            send_row(step, 0).start()

    lag = min(4, units)

    def advance(n, carry):
        @pl.when(n < units)
        def _():
            feed(n)

        @pl.when(n >= lag)
        def _():
            blend(n - lag)

        return carry

    lax.fori_loop(0, units + lag, advance, 0)
    here = pl.ds(pl.multiple_of(tile * cols, lanes), cols)
    out_ref[:, :, here] = merged[0, own_place]

    for mask in range(tile_count - 1, 0, -1):
        take_row(mask).wait_recv()
    for step in steps:
        for mask in range(1, depth_count):
            send(step, mask).wait_send()
    for mask in range(1, tile_count):
        send_row(mask // owners, mask % owners).wait_send()


def local(voxel_bins, colors, opacity, slab_order):
    depth_count = lax.axis_size("depth")
    tile_count = lax.axis_size("screen")
    samples, row_count, cols = voxel_bins.shape
    rows_each = row_count // (depth_count * tile_count)
    unit_rows = max(8, rows_each)
    owners = unit_rows // rows_each
    units = tile_count // owners
    rate = extinction / (samples * depth_count)
    sizes = (depth_count, tile_count, samples, unit_rows, units, owners, rows_each, cols, rate)
    others = depth_count - 1
    vmem = pl.BlockSpec(memory_space=pltpu.VMEM)
    return pl.pallas_call(
        functools.partial(kernel, sizes),
        out_shape=pltpu.VMEM((4, rows_each, cols * tile_count), jnp.float32),
        in_specs=[
            pl.BlockSpec(memory_space=pltpu.SMEM),
            pl.BlockSpec(memory_space=pl.ANY),
            vmem,
            vmem,
        ],
        out_specs=vmem,
        scratch_shapes=[
            pltpu.VMEM((units, depth_count, samples, unit_rows, cols), jnp.int32),
            pltpu.VMEM((units, others, 4, unit_rows, cols), jnp.float32),
            pltpu.VMEM((units, 4, unit_rows, cols), jnp.float32),
            pltpu.VMEM((units, others, 4, unit_rows, cols), jnp.float32),
            pltpu.VMEM((units, owners, 4, rows_each, cols), jnp.float32),
            pltpu.SemaphoreType.DMA((units, depth_count)),
            pltpu.SemaphoreType.DMA((units, others)),
            pltpu.SemaphoreType.DMA((units, others)),
            pltpu.SemaphoreType.DMA((tile_count,)),
            pltpu.SemaphoreType.DMA((tile_count,)),
            pltpu.SemaphoreType.REGULAR,
            pltpu.SemaphoreType.REGULAR,
        ],
        compiler_params=pltpu.CompilerParams(collective_id=0, has_side_effects=True),
    )(slab_order.T, voxel_bins, colors, opacity)


def solution(mesh):
    placed = (P("depth", None, "screen"), P(), P(), P())
    return jax.shard_map(
        local,
        mesh=mesh,
        in_specs=placed,
        out_specs=P(None, ("depth", "screen"), None),
        check_vma=False,
    )
```

profile of v0, /device:TPU:0, one launch (start us, length us, event | category | flops | bytes accessed | tf_op | source)
XLA Modules:
  0.0 21.1 jit_solution(14870779947774251073)
XLA Ops:
  0.0 20.4 %shard_map.46 = f32[4,8,2048]{2,1,0:T(8,128)S(1)} custom-call(s32[4,8]{1,0:T(4,128)} %bitcast.1, s32[8,256,256]{2,1,0:T(8,128)} %bins_hbm.1, bf16[3,256]{1,0:T(4,128)(2,1)} %colors_ref.1, bf16[256]{0:T(256)(128)(2,1)} %opacity_ref.1), custom_call_target="tpu_custom_call" | custom-call | tf_op jit(solution)/shard_map/pallas_call | solution.py:288
  20.4 0.7 %copy.6 = f32[4,8,2048]{2,1,0:T(8,128)} copy(f32[4,8,2048]{2,1,0:T(8,128)S(1)} %shard_map.46) | data formatting | bytes 524288
where the time goes:
time: 21.3 us; the launch traced here: 21.1 us
  Pallas kernels  20.4 us (96%)
  local copies, waits for them, and re-layouts  0.71 us (3%)
    pallas_call x1, Pallas kernels, local(): pl.pallas_call(functools.partial(kernel, sizes), out_shape=pltpu.VMEM((4,...  20.4 us
    unnamed x1, local copies, waits for them, and re-layouts  0.71 us

commit v1 on v0

--- a/solution.py
+++ b/solution.py
@@ -9,6 +9,7 @@
 
 extinction = 3.0
 lanes = 128
+HEAD, LAG = 2, 4
 MESH = pl.DeviceIdType.MESH
 
 
@@ -44,8 +45,10 @@
     recv_sem,
     row_send_sem,
     row_recv_sem,
-    ready_sem,
-    go_sem,
+    pass_sem,
+    passed,
+    pass_send_sem,
+    pass_recv_sem,
 ):
     depth_count, tile_count, samples, unit_rows, units, owners, rows_each, cols, rate = sizes
     depth = lax.axis_index("depth")
@@ -53,44 +56,42 @@
     own_unit = lax.div(tile, owners)
     own_place = lax.rem(tile, owners)
     steps = list(range(units - 1, -1, -1))
+    crossing = [2] if owners == 1 and units > 3 else []
     peers = [depth_count - 1] + list(range(1, depth_count - 1)) + [0]
 
     barrier = pltpu.get_barrier_semaphore()
-    hub = depth == 0
-    for mask in range(1, depth_count):
+    near = [mask for mask in peers if mask and not mask & (mask - 1)]
+    far = [mask for mask in peers if mask & (mask - 1)]
+    below = tile >= 2
+    above = tile + 2 < tile_count
+    beside = 1 + below.astype(jnp.int32) + above.astype(jnp.int32)
+
+    def greet(sem):
+        def tell(there):
+            pl.semaphore_signal(sem, inc=1, device_id=(depth, there), device_id_type=MESH)
+
+        tell(flip(tile, 1, tile_count))
+
+        @pl.when(below)
+        def _():
+            tell(tile - 2)
+
+        @pl.when(above)
+        def _():
+            tell(tile + 2)
+
+    rounds = tile_count // 2 - 1
+
+    def widen(first, last):
+        for n in range(first, min(last, rounds)):
+            pl.semaphore_wait(pass_sem.at[n], beside)
+            if n + 1 < rounds:
+                greet(pass_sem.at[n + 1])
+
+    for mask in far + near:
         peer = flip(depth, mask, depth_count)
-
-        @pl.when(peer != 0)
-        def _():
-            pl.semaphore_signal(barrier, inc=1, device_id=(peer, tile), device_id_type=MESH)
-
-    def meet_depth():
-        @pl.when(jnp.logical_not(hub))
-        def _():
-            pl.semaphore_wait(barrier, depth_count - 1)
-            pl.semaphore_signal(ready_sem, inc=1, device_id=(0, tile), device_id_type=MESH)
-
-        @pl.when(hub)
-        def _():
-            pl.semaphore_wait(ready_sem, depth_count - 1)
-            for mask in range(1, tile_count):
-                pl.semaphore_signal(
-                    barrier,
-                    inc=1,
-                    device_id=(0, flip(tile, mask, tile_count)),
-                    device_id_type=MESH,
-                )
-
-    def meet_tiles():
-        @pl.when(hub)
-        def _():
-            pl.semaphore_wait(barrier, tile_count - 1)
-            for mask in range(1, depth_count):
-                pl.semaphore_signal(go_sem, inc=1, device_id=(mask, tile), device_id_type=MESH)
-
-        @pl.when(jnp.logical_not(hub))
-        def _():
-            pl.semaphore_wait(go_sem, 1)
+        pl.semaphore_signal(barrier, inc=1, device_id=(peer, tile), device_id_type=MESH)
+    greet(barrier)
 
     def fetch(step, mask):
         row = (flip(depth, mask, depth_count) * units + flip(own_unit, step, units)) * unit_rows
@@ -101,12 +102,16 @@
             bins_sem.at[step, mask],
         )
 
-    for step in steps:
-        for mask in peers:
-            if mask:
+    for mask in far + near:
+        fetch(steps[0], mask).start()
+
+    def fetch_rest():
+        for step in steps[1:2] + crossing + [k for k in steps[2:] if k not in crossing]:
+            for mask in far + near:
                 fetch(step, mask).start()
-    for step in steps:
-        fetch(step, 0).start()
+        for step in crossing + [k for k in steps if k not in crossing]:
+            fetch(step, 0).start()
+
 
     density = opacity_ref[...].astype(jnp.float32).reshape(1, -1)
     weight = 1.0 - jnp.exp(-rate * density)
@@ -181,57 +186,96 @@
             device_id_type=MESH,
         )
 
+    def carry_over(step, mask):
+        return pltpu.make_async_remote_copy(
+            src_ref=sent.at[step, mask - 1] if mask else own.at[step],
+            dst_ref=passed.at[mask],
+            send_sem=pass_send_sem.at[mask],
+            recv_sem=pass_recv_sem.at[mask],
+            device_id=(depth, flip(tile, step, tile_count)),
+            device_id_type=MESH,
+        )
+
+    def hand_on(step, mask):
+        return pltpu.make_async_remote_copy(
+            src_ref=passed.at[mask],
+            dst_ref=arrived.at[step, mask - 1],
+            send_sem=send_sem.at[step, mask - 1],
+            recv_sem=recv_sem.at[step, mask - 1],
+            device_id=(flip(depth, mask, depth_count), tile),
+            device_id_type=MESH,
+        )
+
+    def cross():
+        for step in crossing:
+            for mask in far + near + [0]:
+                fetch(step, mask).wait()
+                march(step, mask, sent.at[step, mask - 1] if mask else own.at[step])
+                carry_over(step, mask).start()
+
     def feed(n):
         step = units - 1 - n
-        for mask in peers:
-            if mask:
+
+        def plain():
+            for mask in far + near:
                 fetch(step, mask).wait()
                 march(step, mask, sent.at[step, mask - 1])
-
-        @pl.when(n == 0)
+                send(step, mask).start()
+
+        if not crossing:
+            plain()
+            return
+        pl.when(step != crossing[0])(plain)
+
+        @pl.when(step == crossing[0])
         def _():
-            meet_depth()
-
-        for mask in peers:
-            if mask:
-                send(step, mask).start()
-
-    place_of = [order_ref[flip(depth, mask, depth_count), tile] for mask in range(depth_count)]
-    ahead = [
-        [jnp.where(place_of[j] < place_of[i], 1.0, 0.0) for j in range(depth_count)]
-        for i in range(depth_count)
-    ]
-
-    def blend(n):
-        step = units - 1 - n
-        fetch(step, 0).wait()
-        march(step, 0, own.at[step])
-
-        @pl.when(n == 0)
-        def _():
-            meet_tiles()
-
-        for mask in peers:
-            if mask:
-                send(step, mask).wait_recv()
+            for mask in far + near:
+                carry_over(crossing[0], mask).wait_recv()
+                hand_on(crossing[0], mask).start()
+
+    def fronts(of_tile):
+        place_of = [
+            order_ref[flip(depth, mask, depth_count), of_tile] for mask in range(depth_count)
+        ]
+        return [
+            [jnp.where(place_of[j] < place_of[i], 1.0, 0.0) for j in range(depth_count)]
+            for i in range(depth_count)
+        ]
+
+    def merge(pieces_at, ahead, put):
         for row in range(0, unit_rows, 8):
             for col in range(0, cols, lanes):
-                window = (slice(row, row + 8), slice(col, col + lanes))
-                pieces = [
-                    own[(step, slice(None)) + window]
-                    if mask == 0
-                    else arrived[(step, mask - 1, slice(None)) + window]
-                    for mask in range(depth_count)
-                ]
+                pieces = pieces_at(row, col)
                 total = None
                 for i in range(depth_count):
                     front = None
                     for j in range(depth_count):
                         if j != i:
-                            passed = 1.0 - ahead[i][j] * pieces[j][3]
-                            front = passed if front is None else front * passed
+                            clear = 1.0 - ahead[i][j] * pieces[j][3]
+                            front = clear if front is None else front * clear
                     lit = [pieces[i][c] if front is None else pieces[i][c] * front for c in range(4)]
                     total = lit if total is None else [t + v for t, v in zip(total, lit)]
+                put(row, col, total)
+
+    ahead = fronts(tile)
+
+    def blend(n):
+        step = units - 1 - n
+
+        def plain():
+            fetch(step, 0).wait()
+            march(step, 0, own.at[step])
+            for mask in far + near:
+                send(step, mask).wait_recv()
+
+            def pieces_at(row, col):
+                window = (slice(None), slice(row, row + 8), slice(col, col + lanes))
+                return [
+                    own[(step,) + window] if mask == 0 else arrived[(step, mask - 1) + window]
+                    for mask in range(depth_count)
+                ]
+
+            def put(row, col, total):
                 for c in range(4):
                     if owners == 1:
                         merged[step, 0, c, row : row + 8, col : col + lanes] = total[c]
@@ -240,36 +284,91 @@
                             merged[step, place, c, :, col : col + lanes] = total[c][
                                 place * rows_each : (place + 1) * rows_each
                             ]
-        for low in range(owners - 1, 0, -1):
-            send_row(step, low).start()
-
-        @pl.when(step > 0)
+
+            merge(pieces_at, ahead, put)
+            for low in range(owners - 1, 0, -1):
+                send_row(step, low).start()
+
+            @pl.when(step > 0)
+            def _():
+                send_row(step, 0).start()
+
+        if not crossing:
+            plain()
+            return
+        pl.when(step != crossing[0])(plain)
+
+        @pl.when(step == crossing[0])
         def _():
-            send_row(step, 0).start()
-
-    lag = min(4, units)
+            there = flip(tile, crossing[0], tile_count)
+            carry_over(crossing[0], 0).wait_recv()
+            for mask in far + near:
+                hand_on(crossing[0], mask).wait_recv()
+
+            def pieces_at(row, col):
+                window = (slice(None), slice(row, row + 8), slice(col, col + lanes))
+                return [
+                    passed[(mask,) + window]
+                    if mask == 0
+                    else arrived[(crossing[0], mask - 1) + window]
+                    for mask in range(depth_count)
+                ]
+
+            def put(row, col, total):
+                at = pl.ds(pl.multiple_of(there * cols + col, lanes), lanes)
+                for c in range(4):
+                    out_ref[c, row : row + 8, at] = total[c]
+
+            merge(pieces_at, fronts(there), put)
+
+    def each(first, last, body):
+        def step(n, carry):
+            body(n)
+            return carry
+
+        lax.fori_loop(first, last, step, 0)
+
+    lag = min(LAG, units)
+    for at, mask in enumerate(far + near):
+        fetch(steps[0], mask).wait()
+        if at == 0:
+            fetch_rest()
+        march(steps[0], mask, sent.at[steps[0], mask - 1])
+        if at == 0:
+            pl.semaphore_wait(barrier, depth_count - 1 + beside)
+            if rounds:
+                greet(pass_sem.at[0])
+        send(steps[0], mask).start()
+    each(1, HEAD, feed)
+    widen(0, 1)
+    cross()
+    widen(1, 2)
+    each(HEAD, lag, feed)
+    widen(2, rounds)
 
     def advance(n, carry):
+        blend(n - lag)
+
         @pl.when(n < units)
         def _():
             feed(n)
 
-        @pl.when(n >= lag)
-        def _():
-            blend(n - lag)
-
         return carry
 
-    lax.fori_loop(0, units + lag, advance, 0)
+    lax.fori_loop(lag, units + lag, advance, 0)
     here = pl.ds(pl.multiple_of(tile * cols, lanes), cols)
     out_ref[:, :, here] = merged[0, own_place]
 
-    for mask in range(tile_count - 1, 0, -1):
+    late = [mask for mask in range(tile_count - 1, 0, -1) if mask not in crossing]
+    for mask in late:
         take_row(mask).wait_recv()
     for step in steps:
         for mask in range(1, depth_count):
             send(step, mask).wait_send()
-    for mask in range(1, tile_count):
+    for step in crossing:
+        for mask in range(depth_count):
+            carry_over(step, mask).wait_send()
+    for mask in late:
         send_row(mask // owners, mask % owners).wait_send()
 
 
@@ -306,8 +405,10 @@
             pltpu.SemaphoreType.DMA((units, others)),
             pltpu.SemaphoreType.DMA((tile_count,)),
             pltpu.SemaphoreType.DMA((tile_count,)),
-            pltpu.SemaphoreType.REGULAR,
-            pltpu.SemaphoreType.REGULAR,
+            pltpu.SemaphoreType.REGULAR((tile_count,)),
+            pltpu.VMEM((depth_count, 4, unit_rows, cols), jnp.float32),
+            pltpu.SemaphoreType.DMA((depth_count,)),
+            pltpu.SemaphoreType.DMA((depth_count,)),
         ],
         compiler_params=pltpu.CompilerParams(collective_id=0, has_side_effects=True),
     )(slab_order.T, voxel_bins, colors, opacity)

time: 21.3 us -> 20 us (0.939)
  Pallas kernels: 20.4 us -> 19.1 us
    pallas_call x1, Pallas kernels: 20.4 us -> 19.1 us  [local(): pl.pallas_call(functools.partial(kernel, sizes), out_shape=pltpu.VMEM((4,...]
where the time goes in v1:
time: 20 us; the launch traced here: 19.8 us
  Pallas kernels  19.1 us (96%)
  local copies, waits for them, and re-layouts  0.71 us (4%)
    pallas_call x1, Pallas kernels, local(): pl.pallas_call(functools.partial(kernel, sizes), out_shape=pltpu.VMEM((4,...  19.1 us
    unnamed x1, local copies, waits for them, and re-layouts  0.71 us

profile of v1, /device:TPU:0, one launch (start us, length us, event | category | flops | bytes accessed | tf_op | source)
XLA Modules:
  0.0 19.8 jit_solution(1931930834188464234)
XLA Ops:
  0.0 19.1 %shard_map.46 = f32[4,8,2048]{2,1,0:T(8,128)S(1)} custom-call(s32[4,8]{1,0:T(4,128)} %bitcast.1, s32[8,256,256]{2,1,0:T(8,128)} %bins_hbm.1, bf16[3,256]{1,0:T(4,128)(2,1)} %colors_ref.1, bf16[256]{0:T(256)(128)(2,1)} %opacity_ref.1), custom_call_target="tpu_custom_call" | custom-call | tf_op jit(solution)/shard_map/pallas_call | solution.py:387
  19.1 0.7 %copy.6 = f32[4,8,2048]{2,1,0:T(8,128)} copy(f32[4,8,2048]{2,1,0:T(8,128)S(1)} %shard_map.46) | data formatting | bytes 524288

commit v2 on v1

--- a/solution.py
+++ b/solution.py
@@ -30,11 +30,15 @@
 
 def kernel(
     sizes,
+    order_hbm,
+    bins_hbm,
+    colors_hbm,
+    opacity_hbm,
+    out_ref,
     order_ref,
-    bins_hbm,
     colors_ref,
     opacity_ref,
-    out_ref,
+    table_sem,
     bins,
     sent,
     own,
@@ -102,6 +106,13 @@
             bins_sem.at[step, mask],
         )
 
+    loads = [
+        pltpu.make_async_copy(colors_hbm, colors_ref, table_sem.at[0]),
+        pltpu.make_async_copy(opacity_hbm, opacity_ref, table_sem.at[1]),
+        pltpu.make_async_copy(order_hbm, order_ref, table_sem.at[2]),
+    ]
+    for load in loads:
+        load.start()
     for mask in far + near:
         fetch(steps[0], mask).start()
 
@@ -112,7 +123,8 @@
         for step in crossing + [k for k in steps if k not in crossing]:
             fetch(step, 0).start()
 
-
+    for load in loads:
+        load.wait()
     density = opacity_ref[...].astype(jnp.float32).reshape(1, -1)
     weight = 1.0 - jnp.exp(-rate * density)
     shades = weight * colors_ref[...].astype(jnp.float32)
@@ -383,18 +395,16 @@
     rate = extinction / (samples * depth_count)
     sizes = (depth_count, tile_count, samples, unit_rows, units, owners, rows_each, cols, rate)
     others = depth_count - 1
-    vmem = pl.BlockSpec(memory_space=pltpu.VMEM)
     return pl.pallas_call(
         functools.partial(kernel, sizes),
         out_shape=pltpu.VMEM((4, rows_each, cols * tile_count), jnp.float32),
-        in_specs=[
-            pl.BlockSpec(memory_space=pltpu.SMEM),
-            pl.BlockSpec(memory_space=pl.ANY),
-            vmem,
-            vmem,
-        ],
-        out_specs=vmem,
+        in_specs=[pl.BlockSpec(memory_space=pl.ANY)] * 4,
+        out_specs=pl.BlockSpec(memory_space=pltpu.VMEM),
         scratch_shapes=[
+            pltpu.SMEM(slab_order.shape[::-1], slab_order.dtype),
+            pltpu.VMEM(colors.shape, colors.dtype),
+            pltpu.VMEM(opacity.shape, opacity.dtype),
+            pltpu.SemaphoreType.DMA((3,)),
             pltpu.VMEM((units, depth_count, samples, unit_rows, cols), jnp.int32),
             pltpu.VMEM((units, others, 4, unit_rows, cols), jnp.float32),
             pltpu.VMEM((units, 4, unit_rows, cols), jnp.float32),

time: 20 us -> 19.2 us (0.960)
  Pallas kernels: 19.1 us -> 18.3 us
    pallas_call x1, Pallas kernels: 19.1 us -> 18.3 us  [local(): pl.pallas_call(functools.partial(kernel, sizes), out_shape=pltpu.VMEM((4,...]
where the time goes in v2:
time: 19.2 us; the launch traced here: 19.1 us
  Pallas kernels  18.3 us (95%)
  local copies, waits for them, and re-layouts  0.71 us (4%)
    pallas_call x1, Pallas kernels, local(): pl.pallas_call(functools.partial(kernel, sizes), out_shape=pltpu.VMEM((4,...  18.3 us
    unnamed x1, local copies, waits for them, and re-layouts  0.71 us

profile of v2, /device:TPU:0, one launch (start us, length us, event | category | flops | bytes accessed | tf_op | source)
XLA Modules:
  0.0 19.1 jit_solution(6308449039524375360)
XLA Ops:
  0.0 18.3 %shard_map.46 = f32[4,8,2048]{2,1,0:T(8,128)S(1)} custom-call(s32[4,8]{1,0:T(4,128)} %bitcast.1, s32[8,256,256]{2,1,0:T(8,128)} %bins_hbm.1, bf16[3,256]{1,0:T(4,128)(2,1)} %colors_hbm.1, bf16[256]{0:T(256)(128)(2,1)} %opacity_hbm.1), custom_call_target="tpu_custom_call" | custom-call | tf_op jit(solution)/shard_map/pallas_call | solution.py:398
  18.3 0.7 %copy.6 = f32[4,8,2048]{2,1,0:T(8,128)} copy(f32[4,8,2048]{2,1,0:T(8,128)S(1)} %shard_map.46) | data formatting | bytes 524288

commit v3 on v2

--- a/solution.py
+++ b/solution.py
@@ -9,7 +9,7 @@
 
 extinction = 3.0
 lanes = 128
-HEAD, LAG = 2, 4
+HEAD, LAG, PRE = 3, 4, (6, 3, 1)
 MESH = pl.DeviceIdType.MESH
 
 
@@ -59,8 +59,15 @@
     tile = lax.axis_index("screen")
     own_unit = lax.div(tile, owners)
     own_place = lax.rem(tile, owners)
-    steps = list(range(units - 1, -1, -1))
     crossing = [2] if owners == 1 and units > 3 else []
+    steps = [step for step in range(units - 1, -1, -1) if step not in crossing] + crossing
+
+    def step_of(n):
+        if not crossing:
+            return units - 1 - n
+        kept = jnp.where(n < units - 1 - crossing[0], units - 1 - n, units - 2 - n)
+        return jnp.where(n == units - 1, crossing[0], kept)
+
     peers = [depth_count - 1] + list(range(1, depth_count - 1)) + [0]
 
     barrier = pltpu.get_barrier_semaphore()
@@ -226,7 +233,7 @@
                 carry_over(step, mask).start()
 
     def feed(n):
-        step = units - 1 - n
+        step = step_of(n)
 
         def plain():
             for mask in far + near:
@@ -272,7 +279,7 @@
     ahead = fronts(tile)
 
     def blend(n):
-        step = units - 1 - n
+        step = step_of(n)
 
         def plain():
             fetch(step, 0).wait()
@@ -341,17 +348,28 @@
         lax.fori_loop(first, last, step, 0)
 
     lag = min(LAG, units)
-    for at, mask in enumerate(far + near):
-        fetch(steps[0], mask).wait()
+    ones = sum(lax.rem(lax.div(depth, bit), 2) for bit in near)
+    ready = jnp.where(ones == 0, PRE[0], jnp.where(ones == len(near), PRE[2], PRE[1]))
+    opening = [(step, mask) for step in steps[:2] for mask in far + near]
+    for at, piece in enumerate(opening):
+        fetch(*piece).wait()
         if at == 0:
             fetch_rest()
-        march(steps[0], mask, sent.at[steps[0], mask - 1])
-        if at == 0:
+        march(*piece, sent.at[piece[0], piece[1] - 1])
+
+        @pl.when(ready == at + 1)
+        def _():
             pl.semaphore_wait(barrier, depth_count - 1 + beside)
             if rounds:
                 greet(pass_sem.at[0])
-        send(steps[0], mask).start()
-    each(1, HEAD, feed)
+            for earlier in opening[: at + 1]:
+                send(*earlier).start()
+
+        @pl.when(ready < at + 1)
+        def _():
+            send(*piece).start()
+
+    each(2, HEAD, feed)
     widen(0, 1)
     cross()
     widen(1, 2)

time: 19.2 us -> 18.9 us (0.984)
  Pallas kernels: 18.3 us -> 18 us
    pallas_call x1, Pallas kernels: 18.3 us -> 18 us  [local(): pl.pallas_call(functools.partial(kernel, sizes), out_shape=pltpu.VMEM((4,...]
where the time goes in v3:
time: 18.9 us; the launch traced here: 18.8 us
  Pallas kernels  18 us (95%)
  local copies, waits for them, and re-layouts  0.71 us (4%)
    pallas_call x1, Pallas kernels, local(): pl.pallas_call(functools.partial(kernel, sizes), out_shape=pltpu.VMEM((4,...  18 us
    unnamed x1, local copies, waits for them, and re-layouts  0.71 us

profile of v3, /device:TPU:0, one launch (start us, length us, event | category | flops | bytes accessed | tf_op | source)
XLA Modules:
  0.0 18.8 jit_solution(17429910961092815723)
XLA Ops:
  0.0 18.0 %shard_map.46 = f32[4,8,2048]{2,1,0:T(8,128)S(1)} custom-call(s32[4,8]{1,0:T(4,128)} %bitcast.1, s32[8,256,256]{2,1,0:T(8,128)} %bins_hbm.1, bf16[3,256]{1,0:T(4,128)(2,1)} %colors_hbm.1, bf16[256]{0:T(256)(128)(2,1)} %opacity_hbm.1), custom_call_target="tpu_custom_call" | custom-call | tf_op jit(solution)/shard_map/pallas_call | solution.py:416
  18.0 0.7 %copy.6 = f32[4,8,2048]{2,1,0:T(8,128)} copy(f32[4,8,2048]{2,1,0:T(8,128)S(1)} %shard_map.46) | data formatting | bytes 524288

commit v4 on v3

--- a/solution.py
+++ b/solution.py
@@ -229,14 +229,15 @@
         for step in crossing:
             for mask in far + near + [0]:
                 fetch(step, mask).wait()
+            for mask in far + near + [0]:
                 march(step, mask, sent.at[step, mask - 1] if mask else own.at[step])
                 carry_over(step, mask).start()
 
-    def feed(n):
+    def give(n, masks):
         step = step_of(n)
 
         def plain():
-            for mask in far + near:
+            for mask in masks:
                 fetch(step, mask).wait()
                 march(step, mask, sent.at[step, mask - 1])
                 send(step, mask).start()
@@ -248,9 +249,19 @@
 
         @pl.when(step == crossing[0])
         def _():
-            for mask in far + near:
+            for mask in masks:
                 carry_over(crossing[0], mask).wait_recv()
                 hand_on(crossing[0], mask).start()
+
+    def feed(n):
+        give(n, far + near)
+
+    def feed_ahead(n):
+        @pl.when(n + 1 < units)
+        def _():
+            give(n + 1, far)
+
+        give(n, near)
 
     def fronts(of_tile):
         place_of = [
@@ -374,6 +385,7 @@
     cross()
     widen(1, 2)
     each(HEAD, lag, feed)
+    give(min(lag, units - 1), far) if lag < units else None
     widen(2, rounds)
 
     def advance(n, carry):
@@ -381,7 +393,7 @@
 
         @pl.when(n < units)
         def _():
-            feed(n)
+            feed_ahead(n)
 
         return carry
 

time: 18.9 us -> 18.8 us (level)
  no operation moved by 1% of the time
where the time goes in v4:
time: 18.8 us; the launch traced here: 18.6 us
  Pallas kernels  17.9 us (95%)
  local copies, waits for them, and re-layouts  0.71 us (4%)
    pallas_call x1, Pallas kernels, local(): pl.pallas_call(functools.partial(kernel, sizes), out_shape=pltpu.VMEM((4,...  17.9 us
    unnamed x1, local copies, waits for them, and re-layouts  0.71 us

profile of v4, /device:TPU:0, one launch (start us, length us, event | category | flops | bytes accessed | tf_op | source)
XLA Modules:
  0.0 18.6 jit_solution(4265506998833234517)
XLA Ops:
  0.0 17.9 %shard_map.46 = f32[4,8,2048]{2,1,0:T(8,128)S(1)} custom-call(s32[4,8]{1,0:T(4,128)} %bitcast.1, s32[8,256,256]{2,1,0:T(8,128)} %bins_hbm.1, bf16[3,256]{1,0:T(4,128)(2,1)} %colors_hbm.1, bf16[256]{0:T(256)(128)(2,1)} %opacity_hbm.1), custom_call_target="tpu_custom_call" | custom-call | tf_op jit(solution)/shard_map/pallas_call | solution.py:428
  17.9 0.7 %copy.6 = f32[4,8,2048]{2,1,0:T(8,128)} copy(f32[4,8,2048]{2,1,0:T(8,128)S(1)} %shard_map.46) | data formatting | bytes 524288

commit v5 on v4

--- a/solution.py
+++ b/solution.py
@@ -289,6 +289,21 @@
 
     ahead = fronts(tile)
 
+    late = [mask for mask in range(tile_count - 1, 0, -1) if mask not in crossing]
+
+    def settle():
+        here = pl.ds(pl.multiple_of(tile * cols, lanes), cols)
+        out_ref[:, :, here] = merged[0, own_place]
+        for step in steps:
+            for mask in range(1, depth_count):
+                if step not in crossing:
+                    send(step, mask).wait_send()
+        for step in crossing:
+            for mask in range(depth_count):
+                carry_over(step, mask).wait_send()
+        for mask in late:
+            send_row(mask // owners, mask % owners).wait_send()
+
     def blend(n):
         step = step_of(n)
 
@@ -331,6 +346,7 @@
         @pl.when(step == crossing[0])
         def _():
             there = flip(tile, crossing[0], tile_count)
+            settle()
             carry_over(crossing[0], 0).wait_recv()
             for mask in far + near:
                 hand_on(crossing[0], mask).wait_recv()
@@ -398,20 +414,13 @@
         return carry
 
     lax.fori_loop(lag, units + lag, advance, 0)
-    here = pl.ds(pl.multiple_of(tile * cols, lanes), cols)
-    out_ref[:, :, here] = merged[0, own_place]
-
-    late = [mask for mask in range(tile_count - 1, 0, -1) if mask not in crossing]
+    if not crossing:
+        settle()
     for mask in late:
         take_row(mask).wait_recv()
-    for step in steps:
+    for step in crossing:
         for mask in range(1, depth_count):
             send(step, mask).wait_send()
-    for step in crossing:
-        for mask in range(depth_count):
-            carry_over(step, mask).wait_send()
-    for mask in late:
-        send_row(mask // owners, mask % owners).wait_send()
 
 
 def local(voxel_bins, colors, opacity, slab_order):

time: 18.8 us -> 18.8 us (level)
  no operation moved by 1% of the time
where the time goes in v5:
time: 18.8 us; the launch traced here: 18.6 us
  Pallas kernels  17.9 us (95%)
  local copies, waits for them, and re-layouts  0.71 us (4%)
    pallas_call x1, Pallas kernels, local(): pl.pallas_call(functools.partial(kernel, sizes), out_shape=pltpu.VMEM((4,...  17.9 us
    unnamed x1, local copies, waits for them, and re-layouts  0.71 us

profile of v5, /device:TPU:0, one launch (start us, length us, event | category | flops | bytes accessed | tf_op | source)
XLA Modules:
  0.0 18.6 jit_solution(8836130380098886614)
XLA Ops:
  0.0 17.9 %shard_map.46 = f32[4,8,2048]{2,1,0:T(8,128)S(1)} custom-call(s32[4,8]{1,0:T(4,128)} %bitcast.1, s32[8,256,256]{2,1,0:T(8,128)} %bins_hbm.1, bf16[3,256]{1,0:T(4,128)(2,1)} %colors_hbm.1, bf16[256]{0:T(256)(128)(2,1)} %opacity_hbm.1), custom_call_target="tpu_custom_call" | custom-call | tf_op jit(solution)/shard_map/pallas_call | solution.py:437
  17.9 0.7 %copy.6 = f32[4,8,2048]{2,1,0:T(8,128)} copy(f32[4,8,2048]{2,1,0:T(8,128)S(1)} %shard_map.46) | data formatting | bytes 524288
